TPU v7x, 32 devices: a whole 2x2x4 slice. The times are simulated.
32 devices in a mesh: unit: 4 (over y, core), ep: 4 (over z), fsdp: 2 (over x).
Axes of the slice: x: 2, y: 2, z: 4, core: 2. Of those that a mesh axis runs over, the one named last changes fastest.
Arguments:
- w_down: float32 [256, 1024, 2048], P(('unit', 'ep'), None, 'fsdp'), parts along dimension 0, may hold values from -0.25 to 0.25
- router_weight: float32 [8192, 64], P(('unit', 'fsdp'), 'ep'), parts along dimension 0, may hold values from -0.125 to 0.125
- router_gain: float32 [8192], P(('unit', 'fsdp')), parts along dimension 0, may hold values from 0.25 to 1.75
Outputs:
- serve_down: bfloat16 [256, 1024, 2048], P(('unit', 'ep'), 'fsdp'), parts along dimension 0
- scale_down: float32 [256, 1024], P(('unit', 'ep'), 'fsdp'), parts along dimension 0
- serve_router: bfloat16 [8192, 64], P('unit'), parts along dimension 0
There are 4 independent parts, one for each index of `unit`. A program takes and returns all parts, laid end to end along the dimension named above; each array names one. Nothing has to cross between parts.
All inputs are finite; a program needn't handle non-finite values. Where the computation divides by a largest or mean magnitude, that divisor is 1e-20 or more.
Results may differ from a plain program's by a relative error of at most 0.001.
Values may be sent and summed in bfloat16 or wider, within the bound.
A program may use at most 256 MiB of HBM per device.

v0:
```python
import jax
import jax.numpy as jnp
from jax import lax
from jax.sharding import PartitionSpec as P

D_MODEL = 2048


def on_device(w_down, router_weight, router_gain):
    total_down = lax.psum(jnp.sum(jnp.abs(w_down), axis=2), "fsdp")
    scale_down = total_down / D_MODEL
    narrow_down = (w_down / jnp.expand_dims(scale_down, 2)).astype(jnp.bfloat16)
    serve_down = lax.all_to_all(narrow_down, "fsdp", split_axis=1, concat_axis=2, tiled=True)
    scale_down = lax.dynamic_slice_in_dim(
        scale_down, lax.axis_index("fsdp") * serve_down.shape[1], serve_down.shape[1], axis=1
    )
    part_router = (router_weight * router_gain[:, None]).astype(jnp.bfloat16)
    row_router = lax.all_gather(part_router, "fsdp", axis=0, tiled=True)
    serve_router = lax.all_gather(row_router, "ep", axis=1, tiled=True)
    return (serve_down, scale_down, serve_router)


def solution(mesh):
    return jax.shard_map(
        on_device,
        mesh=mesh,
        in_specs=(P(("unit", "ep"), None, "fsdp"), P(("unit", "fsdp"), "ep"), P(("unit", "fsdp"))),
        out_specs=(P(("unit", "ep"), "fsdp", None), P(("unit", "ep"), "fsdp"), P("unit", None)),
        check_vma=False,
    )
```

profile of v0, /device:TPU:0, one launch (start us, length us, event | category | flops | bytes accessed | tf_op | source)
XLA Modules:
  0.0 625.7 jit_solution(12388147618959563152)
XLA Ops:
  7.2 0.0 all-reduce.2.cloned.1.call-start
  7.2 21.4 %abs_reduce_fusion = f32[16,1024]{1,0:T(8,128)} fusion(f32[16,1024,1024]{2,1,0:T(8,128)} %param.3), kind=kLoop, calls=%fused_computation.2 | loop fusion | flops 33538048 | bytes 67174400 | tf_op jit(solution)/shard_map/reduce_sum | solution.py:10
  28.6 0.0 all-reduce.2.cloned.1.call-update
  28.7 23.8 %all-reduce.2.cloned.1.call-done = f32[16,1024]{1,0:T(8,128)} async-done(((f32[16,1024]{1,0:T(8,128)}), f32[16,1024]{1,0:T(8,128)}) %all-reduce.2.cloned.1.call-update) | async-done | bytes 65552 | tf_op jit(solution)/shard_map/psum | solution.py:10
  52.5 0.8 broadcast_multiply_fusion
  53.3 0.2 copy.7
  53.5 0.0 copy-start
  53.5 0.0 copy-start.1
  53.6 60.1 %fusion = bf16[16,1024,1024]{2,0,1:T(8,128)(2,1)} fusion(f32[16,1024,1024]{2,1,0:T(8,128)} %param.3, f32[16,1024]{0,1:T(8,128)S(1)} %copy.7), kind=kLoop, calls=%fused_computation.1 | loop fusion | flops 33554432 | bytes 100728832 | tf_op jit(solution)/shard_map/convert_element_type | solution.py:12
  113.7 13.0 %all-to-all-start = ((bf16[16,1024,1024]{2,0,1:T(8,128)(2,1)}), bf16[16,1024,1024]{2,0,1:T(8,128)(2,1)}, u32[]{:S(2)}, u32[]{:S(2)}) async-start(bf16[16,1024,1024]{2,0,1:T(8,128)(2,1)} %fusion), calls=%async_computation | async-start | bytes 67108864 | tf_op jit(solution)/shard_map/all_to_all | solution.py:13
  126.6 0.0 copy-done
  126.6 0.0 copy-done.1
  126.7 362.4 %all_gather.6 = bf16[2048,16]{0,1:T(8,128)(2,1)S(1)} all-gather(bf16[1024,16]{0,1:T(8,128)(2,1)S(1)} %multiply_convert_fusion), channel_id=1, replica_groups=mesh['unit'=4,'ep'=4,'fsdp'=2] {'fsdp'}, dimensions={0}, use_global_device_ids=true | all-gather | bytes 98304 | tf_op jit(solution)/shard_map/all_gather | solution.py:18
  489.0 13.8 %all_gather.7 = bf16[2048,64]{0,1:T(8,128)(2,1)S(1)} all-gather(bf16[2048,16]{0,1:T(8,128)(2,1)S(1)} %all_gather.6), channel_id=1, replica_groups=mesh['unit'=4,'ep'=4,'fsdp'=2] {'ep'}, dimensions={1}, use_global_device_ids=true | all-gather | bytes 327680 | tf_op jit(solution)/shard_map/all_gather | solution.py:19
  502.9 0.6 constant_dynamic-slice_fusion
  503.5 0.0 all-to-all-done
  503.5 60.5 %copy.9 = bf16[16,512,2,1024]{3,2,1,0:T(2,128)(2,1)} copy(bf16[16,512,2,1024]{3,0,1,2:T(8,128)(2,1)} %bitcast.1) | data formatting | bytes 67108864 | tf_op jit(solution)/shard_map/all_to_all | solution.py:13
  564.0 54.2 %all_to_all.16 = bf16[16,512,2048]{2,1,0:T(8,128)(2,1)} reshape(bf16[16,512,2,1024]{3,2,1,0:T(2,128)(2,1)} %copy.9) | data formatting | bytes 67108864 | tf_op jit(solution)/shard_map/all_to_all | solution.py:13
  618.2 0.7 copy.15
  (1 shorter events, 0.0 us)
Async XLA Ops:
  7.2 45.3 %all-reduce.2.cloned.1.call-start = ((), (), s32[]{:S(2)}) async-start(), calls=%async_computation.1 | async-start | bytes 131072 | tf_op jit(solution)/shard_map/psum | solution.py:10
  53.5 73.1 %copy-start = (f32[1024,16]{0,1:T(8,128)S(1)}, f32[1024,16]{0,1:T(8,128)}, u32[]{:S(2)}) copy-start(f32[1024,16]{0,1:T(8,128)} %param.4) | copy-start | bytes 196612
  53.5 73.1 %copy-start.1 = (f32[1024]{0:T(1024)S(1)}, f32[1024]{0:T(1024)}, u32[]{:S(2)}) copy-start(f32[1024]{0:T(1024)} %param.5) | copy-start | bytes 12292
  113.7 389.8 %all-to-all-start = ((bf16[16,1024,1024]{2,0,1:T(8,128)(2,1)}), bf16[16,1024,1024]{2,0,1:T(8,128)(2,1)}, u32[]{:S(2)}, u32[]{:S(2)}) async-start(bf16[16,1024,1024]{2,0,1:T(8,128)(2,1)} %fusion), calls=%async_computation | async-start | bytes 67108864 | tf_op jit(solution)/shard_map/all_to_all | solution.py:13
Sparse Core Ops, SparseCore 0:
  28.8 23.6 all-reduce.1
where the time goes:
time: 627 us; the launch traced here: 626 us
  blocking collectives  376 us (60%)
  local copies, waits for them, and re-layouts  116 us (19%)
  other arithmetic  82.4 us (13%)
  waiting for transfers between devices  23.9 us (4%)
  between operations  14.1 us (2%)
  starting transfers between devices  13 us (2%)
    all_gather x1, blocking collectives, on_device(): row_router = lax.all_gather(part_router, 'fsdp', axis=0, tiled=True)  362 us
    all_to_all x2, local copies, waits for them, and re-layouts, on_device(): lax.all_to_all(narrow_down, 'fsdp', split_axis=1, concat_axis=2, tiled=True)  115 us
    convert_element_type x1, other arithmetic, on_device(): narrow_down = (w_down / jnp.expand_dims(scale_down, 2)).astype(jnp.bfloat16)  60.1 us
    psum x1, waiting for transfers between devices, on_device(): total_down = lax.psum(jnp.sum(jnp.abs(w_down), axis=2), 'fsdp')  23.8 us
    reduce_sum x1, other arithmetic, on_device(): total_down = lax.psum(jnp.sum(jnp.abs(w_down), axis=2), 'fsdp')  21.4 us
    all_gather x1, blocking collectives, on_device(): serve_router = lax.all_gather(row_router, 'ep', axis=1, tiled=True)  13.8 us
    all_to_all x1, starting transfers between devices, on_device(): lax.all_to_all(narrow_down, 'fsdp', split_axis=1, concat_axis=2, tiled=True)  13 us
  transfers between devices with their start and end apart: 2, of which 1 were waited for; matrix products, arithmetic and copies ran while one was open for 0% of the time, Pallas kernels for 0%

commit v1 on v0

v1 whole, which is shorter than its diff:
```python
import functools

import jax
import jax.numpy as jnp
from jax import lax
from jax.experimental import pallas as pl
from jax.experimental.pallas import tpu as pltpu
from jax.sharding import PartitionSpec as P


LANES = 128
PARAMS = pltpu.CompilerParams(vmem_limit_bytes=67043328)


def cost(read, written):
    return pl.CostEstimate(flops=0, bytes_accessed=read + written, transcendentals=0)


def sums_kernel(place_ref, w_ref, *refs):
    out_ref = refs[-1]
    _, columns = w_ref.shape[1:]
    total = jnp.abs(w_ref[0, :, :LANES])
    for at in range(LANES, columns, LANES):
        total = total + jnp.abs(w_ref[0, :, at : at + LANES])
    out_ref[0] = jnp.sum(total.T, axis=0, keepdims=True)


def sums(place, w, first, count, after, step):
    rows, columns = w.shape[1:]
    step = min(rows, step)
    return pl.pallas_call(
        sums_kernel,
        grid_spec=pltpu.PrefetchScalarGridSpec(
            num_scalar_prefetch=1,
            grid=(count, rows // step),
            in_specs=[pl.BlockSpec((1, step, columns), lambda e, r, p: (first + e, r, 0))]
            + [pl.BlockSpec(memory_space=pl.ANY)] * len(after),
            out_specs=pl.BlockSpec((1, 1, step), lambda e, r, p: (e, 0, r)),
        ),
        out_shape=jax.ShapeDtypeStruct((count, 1, rows), jnp.float32),
        compiler_params=PARAMS,
        cost_estimate=cost(4 * count * rows * columns, 4 * count * rows),
        name="sums",
    )(place, w, *after)


def inverse_column(parts, width):
    total = parts[0][0, 0]
    for part in parts[1:]:
        total = total + part[0, 0]
    inverse = 1.0 / (total * (1.0 / width))
    return jnp.broadcast_to(inverse, (LANES, inverse.shape[1])).T


def scaled(w_ref, inverse, put):
    for at in range(0, w_ref.shape[2], LANES):
        put(at, (w_ref[0, :, at : at + LANES] * inverse).astype(jnp.bfloat16))


def narrow_kernel(n, held, width, place_ref, *refs):
    for s in range(n - 1):
        w_ref, parts = refs[s * (held + 1)], refs[s * (held + 1) + 1 : (s + 1) * (held + 1)]
        out_ref = refs[len(refs) - (n - 1) + s]

        def put(at, value):
            out_ref[0, :, at : at + LANES] = value

        scaled(w_ref, inverse_column(parts, width), put)


def narrow(n, place, w, parts, width, first, count, base, after):
    rows, columns = w.shape[1] // n, w.shape[2]
    parts = [part.reshape(part.shape[0], n, 1, rows) for part in parts]
    in_specs, operands = [], []
    for s in range(1, n):
        in_specs.append(
            pl.BlockSpec((1, rows, columns), lambda e, p, s=s: (first + e, lax.rem(p[0] + s, n), 0))
        )
        in_specs += [
            pl.BlockSpec((1, 1, 1, rows), lambda e, p, s=s: (first - base + e, lax.rem(p[0] + s, n), 0, 0))
        ] * len(parts)
        operands += [w, *parts]
    shape = jax.ShapeDtypeStruct((count, rows, columns), jnp.bfloat16)
    return pl.pallas_call(
        functools.partial(narrow_kernel, n, len(parts), width),
        grid_spec=pltpu.PrefetchScalarGridSpec(
            num_scalar_prefetch=1,
            grid=(count,),
            in_specs=in_specs + [pl.BlockSpec(memory_space=pl.ANY)] * len(after),
            out_specs=[pl.BlockSpec((1, rows, columns), lambda e, p: (e, 0, 0))] * (n - 1),
        ),
        out_shape=[shape] * (n - 1),
        compiler_params=PARAMS,
        cost_estimate=cost(4 * count * (n - 1) * rows * columns, 2 * count * (n - 1) * rows * columns),
        name="narrow",
    )(place, *operands, *after)


def join_kernel(n, held, width, place_ref, w_ref, *refs):
    parts, arrived, out_ref = refs[:held], refs[held : held + n - 1], refs[-1]
    columns = w_ref.shape[2]
    me = place_ref[0]

    def put(at, value):
        out_ref[0, :, pl.ds(pl.multiple_of(me * columns + at, LANES), LANES)] = value

    scaled(w_ref, inverse_column(parts, width), put)
    for s in range(1, n):
        source = lax.rem(me + s, n)
        out_ref[0, :, pl.ds(pl.multiple_of(source * columns, LANES), columns)] = arrived[s - 1][0]


def join(n, place, w, parts, arrived, width, first, count, base, out):
    rows, columns = w.shape[1] // n, w.shape[2]
    parts = [part.reshape(part.shape[0], n, 1, rows) for part in parts]
    in_specs = [pl.BlockSpec((1, rows, columns), lambda e, p: (first + e, p[0], 0))]
    in_specs += [pl.BlockSpec((1, 1, 1, rows), lambda e, p: (first - base + e, p[0], 0, 0))] * len(parts)
    in_specs += [pl.BlockSpec((1, rows, columns), lambda e, p: (e, 0, 0))] * (n - 1)
    operands = [place, w, *parts, *arrived]
    aliases = {}
    if out is not None:
        in_specs.append(pl.BlockSpec(memory_space=pl.ANY))
        aliases = {len(operands): 0}
        operands.append(out)
    return pl.pallas_call(
        functools.partial(join_kernel, n, len(parts), width),
        grid_spec=pltpu.PrefetchScalarGridSpec(
            num_scalar_prefetch=1,
            grid=(count,),
            in_specs=in_specs,
            out_specs=pl.BlockSpec((1, rows, n * columns), lambda e, p: (first + e, 0, 0)),
        ),
        out_shape=jax.ShapeDtypeStruct((w.shape[0], rows, n * columns), jnp.bfloat16),
        input_output_aliases=aliases,
        compiler_params=PARAMS,
        cost_estimate=cost((4 + 2 * (n - 1)) * count * rows * columns, 2 * n * count * rows * columns),
        name="join",
    )(*operands)


def own_kernel(width, place_ref, w_ref, *refs):
    out_ref = refs[-1]

    def put(at, value):
        out_ref[0, :, at : at + LANES] = value

    scaled(w_ref, inverse_column(refs[:-1], width), put)


def own(n, place, w, parts, width, first, count, base):
    rows, columns = w.shape[1] // n, w.shape[2]
    parts = [part.reshape(part.shape[0], n, 1, rows) for part in parts]
    return pl.pallas_call(
        functools.partial(own_kernel, width),
        grid_spec=pltpu.PrefetchScalarGridSpec(
            num_scalar_prefetch=1,
            grid=(count,),
            in_specs=[pl.BlockSpec((1, rows, columns), lambda e, p: (first + e, p[0], 0))]
            + [pl.BlockSpec((1, 1, 1, rows), lambda e, p: (first - base + e, p[0], 0, 0))] * len(parts),
            out_specs=pl.BlockSpec((1, rows, columns), lambda e, p: (first + e, 0, p[0])),
        ),
        out_shape=jax.ShapeDtypeStruct((w.shape[0], rows, n * columns), jnp.bfloat16),
        compiler_params=PARAMS,
        cost_estimate=cost(4 * count * rows * columns, 2 * count * rows * columns),
        name="own",
    )(place, w, *parts)


def lay_kernel(place_ref, block_ref, *refs):
    refs[-1][...] = block_ref[...]


def lay(n, place, arrived, s, first, out, after):
    count, rows, columns = arrived.shape
    return pl.pallas_call(
        lay_kernel,
        grid_spec=pltpu.PrefetchScalarGridSpec(
            num_scalar_prefetch=1,
            grid=(count,),
            in_specs=[pl.BlockSpec((1, rows, columns), lambda e, p: (e, 0, 0))]
            + [pl.BlockSpec(memory_space=pl.ANY)] * (1 + len(after)),
            out_specs=pl.BlockSpec((1, rows, columns), lambda e, p: (first + e, 0, lax.rem(p[0] + s, n))),
        ),
        out_shape=jax.ShapeDtypeStruct(out.shape, out.dtype),
        input_output_aliases={2: 0},
        compiler_params=PARAMS,
        cost_estimate=cost(2 * count * rows * columns, 2 * count * rows * columns),
        name="lay",
    )(place, arrived, out, *after)


def settle_kernel(router_ref, out_ref):
    out_ref[...] = router_ref[...]


def settle(router):
    return pl.pallas_call(
        settle_kernel,
        out_shape=jax.ShapeDtypeStruct(router.shape, router.dtype),
        compiler_params=PARAMS,
        cost_estimate=cost(2 * router.size, 2 * router.size),
        name="settle",
    )(router)


def exchange(value_of, n):
    got = [None] * n
    for s in range(1, n):
        got[n - s] = lax.ppermute(value_of(s), "fsdp", [(i, (i + s) % n) for i in range(n)])
    return got[1:]


def plan_of(experts):
    if experts < 8:
        return [1] * experts, [experts]
    middle = experts - 4
    thirds = [middle // 3 + (i < middle % 3) for i in range(3)]
    return [1, 1, 1] + thirds + [1], [1, 2, 4]


def swapped(n, part):
    got = exchange(lambda s: part, n)
    return [part] + got if n <= 2 else [sum(got, part)]


def on_device(n, w_down, router_weight, router_gain):
    return steps(n, w_down, router_weight, router_gain)


def steps(n, w_down, router_weight, router_gain):
    experts, rows, columns = w_down.shape
    width = n * columns
    me = lax.axis_index("fsdp")
    place = jnp.reshape(me, (1,)).astype(jnp.int32)

    chunks, groups = plan_of(experts)
    firsts = [sum(chunks[:at]) for at in range(len(chunks))]
    parts_of, sent, arrived = [], [], []
    totals = []

    def group(at):
        begin = sum(groups[:at])
        base, count = firsts[begin], sum(chunks[begin : begin + groups[at]])
        after = tuple(sent[-1]) if at == 2 else (totals[0],) if at == 1 else ()
        part = sums(place, w_down, base, count, after, 512 if at == 0 else 1024)
        totals.append(part)
        parts_of.extend([(base, swapped(n, part))] * groups[at])

    group(0)
    if len(groups) > 1:
        group(1)
    for at, count in enumerate(chunks):
        if at == 2 and len(groups) > 2:
            group(2)
        base, parts = parts_of[at]
        after = tuple(sent[-1]) if sent else ()
        if at == 2:
            after += (totals[-1],)
        out = narrow(n, place, w_down, parts, width, firsts[at], count, base, after)
        sent.append(out)
        arrived.append(exchange(lambda s: out[s - 1], n))

    if n > 1:
        router_weight, _ = lax.optimization_barrier((router_weight, sent[0][0]))
    part_router = (router_weight.T * router_gain[None, :]).astype(jnp.bfloat16)
    routers = [part_router] + exchange(lambda s: part_router, n)
    slots = []
    for source in range(n):
        piece = routers[0]
        for s in range(1, n):
            piece = jnp.where((me + s) % n == source, routers[s], piece)
        slots.append(piece)
    row_router = jnp.concatenate(slots, axis=1)
    if n > 1:
        row_router, _ = lax.optimization_barrier((row_router, sent[-1][0]))
    serve_router = settle(lax.all_gather(row_router, "ep", axis=0, tiled=True))

    last = len(chunks) - 1
    base, parts = parts_of[last]
    serve_down = own(n, place, w_down, parts, width, firsts[last], chunks[last], base)
    for at in range(last):
        base, parts = parts_of[at]
        serve_down = join(n, place, w_down, parts, arrived[at], width, firsts[at], chunks[at], base, serve_down)
    for s in range(1, n):
        serve_down = lay(n, place, arrived[last][s - 1], s, firsts[last], serve_down, (serve_router,))

    whole, seen = [], 0
    for size in groups:
        parts = parts_of[seen][1]
        whole.append(sum(parts[1:], parts[0]))
        seen += size
    scale_down = jnp.concatenate(whole, axis=0)[:, 0] / width
    scale_down = lax.dynamic_slice_in_dim(scale_down, me * (rows // n), rows // n, axis=1)
    return (serve_down, scale_down, serve_router.T)


def solution(mesh):
    n = mesh.shape["fsdp"]

    def whole(w_down, router_weight, router_gain):
        step = jax.shard_map(
            functools.partial(on_device, n),
            mesh=mesh,
            in_specs=(P(("unit", "ep"), None, "fsdp"), P(("unit", "fsdp"), "ep"), P(("unit", "fsdp"))),
            out_specs=(P(("unit", "ep"), "fsdp", None), P(("unit", "ep"), "fsdp"), P("unit", None)),
            check_vma=False,
        )
        return step(w_down, router_weight, router_gain)

    return whole
```

time: 627 us -> 438 us (0.70)
  blocking collectives: 376 us -> 16.6 us
  waiting for transfers between devices: 23.9 us -> 303 us
  local copies, waits for them, and re-layouts: 116 us -> 1.23 us
  Pallas kernels: 0 us -> 101 us
  other arithmetic: 82.4 us -> 6.54 us
  between operations: 14.1 us -> 0.67 us
    all_gather x2 -> x1, blocking collectives: 376 us -> 16.6 us  [steps(): serve_router = settle(lax.all_gather(row_router, 'ep', axis=0, tiled=True))]
    ppermute x0 -> x11, waiting for transfers between devices: none -> 303 us  [exchange(): lax.ppermute(value_of(s), 'fsdp', [(i, (i + s) % n) for i in range(n)])]
    all_to_all x2 -> x0, local copies, waits for them, and re-layouts: 115 us -> none  [on_device(): lax.all_to_all(narrow_down, 'fsdp', split_axis=1, concat_axis=2, tiled=True)]
    pallas_call x0 -> x19, Pallas kernels: none -> 101 us  [the longest x6 36.8 us: join(): pl.pallas_call(functools.partial(join_kernel, n, len(parts), width), grid...]
    convert_element_type x2 -> x1, other arithmetic: 60.1 us -> 0.85 us  [steps(): part_router = (router_weight.T * router_gain[None, :]).astype(jnp.bfloat16)]
    psum x1 -> x0, waiting for transfers between devices: 23.8 us -> none  [on_device(): total_down = lax.psum(jnp.sum(jnp.abs(w_down), axis=2), 'fsdp')]
    reduce_sum x1 -> x0, other arithmetic: 21.4 us -> none  [on_device(): total_down = lax.psum(jnp.sum(jnp.abs(w_down), axis=2), 'fsdp')]
    all_to_all x1 -> x0, starting transfers between devices: 13 us -> none  [on_device(): lax.all_to_all(narrow_down, 'fsdp', split_axis=1, concat_axis=2, tiled=True)]
  transfers between devices with their start and end apart: 2 -> 11, of which waited for: 1 -> 5; matrix products, arithmetic and copies ran while one was open for 0% -> 2% of each run, Pallas kernels for 0% -> 14%
where the time goes in v1:
time: 438 us; the launch traced here: 437 us
  waiting for transfers between devices  303 us (69%)
  Pallas kernels  101 us (23%)
  blocking collectives  16.6 us (4%)
  starting transfers between devices  8.86 us (2%)
  other arithmetic  6.54 us (1%)
    ppermute x11, waiting for transfers between devices, exchange(): lax.ppermute(value_of(s), 'fsdp', [(i, (i + s) % n) for i in range(n)])  303 us
    pallas_call x6, Pallas kernels, join(): pl.pallas_call(functools.partial(join_kernel, n, len(parts), width), grid...  36.8 us
    pallas_call x7, Pallas kernels, narrow(): pl.pallas_call(functools.partial(narrow_kernel, n, len(parts), width), gr...  29.8 us
    pallas_call x3, Pallas kernels, sums(): pl.pallas_call(sums_kernel, grid_spec=pltpu.PrefetchScalarGridSpec(num_sc...  27.5 us
    all_gather x1, blocking collectives, steps(): serve_router = settle(lax.all_gather(row_router, 'ep', axis=0, tiled=True))  16.6 us
    ppermute x11, starting transfers between devices, exchange(): lax.ppermute(value_of(s), 'fsdp', [(i, (i + s) % n) for i in range(n)])  8.86 us
  transfers between devices with their start and end apart: 11, of which 5 were waited for; matrix products, arithmetic and copies ran while one was open for 2% of the time, Pallas kernels for 14%

profile of v1, /device:TPU:0, one launch (start us, length us, event | category | flops | bytes accessed | tf_op | source)
XLA Modules:
  0.0 437.3 jit_solution(2713230257502056778)
XLA Ops:
  0.6 3.1 sums.3.refs_0_
  3.7 4.4 %sums.4 = f32[2,1,1024]{2,1,0:T(1,128)} custom-call(s32[1]{0:T(128)} %bitcast.place_ref, f32[16,1024,1024]{2,1,0:T(8,128)} %w_ref.19, f32[1,1,1024]{2,1,0:T(1,128)} %sums.3.refs_0_), custom_call_target="tpu_custom_call" | custom-call | bytes 8396800 | tf_op jit(solution)/shard_map/sums/pallas_call | solution.py:31
  8.1 3.0 collective-permute-start
  11.1 3.9 collective-permute-done.1
  15.0 2.8 narrow.7.refs_3_
  17.8 2.8 narrow.8.refs_0_.refs_3_
  20.6 20.1 %sums.5.refs_4_ = f32[13,1,1024]{2,1,0:T(1,128)} custom-call(s32[1]{0:T(128)} %bitcast.place_ref, f32[16,1024,1024]{2,1,0:T(8,128)} %w_ref.19, bf16[1,512,1024]{2,1,0:T(8,128)(2,1)} %narrow.8.refs_0_.refs_3_), custom_call_target="tpu_custom_call" | custom-call | bytes 54579200 | tf_op jit(solution)/shard_map/sums/pallas_call | solution.py:31
  40.8 2.8 narrow.9.refs_3_
  45.1 6.1 %narrow.10.refs_3_ = bf16[4,512,1024]{2,1,0:T(8,128)(2,1)} custom-call(s32[1]{0:T(128)} %bitcast.place_ref, f32[16,1024,1024]{2,1,0:T(8,128)} %w_ref.19, f32[13,2,1,512]{3,2,1,0:T(1,128)} %bitcast.15, f32[13,2,1,512]{3,2,1,0:T(1,128)} %bitcast.6.refs_2_.refs_1_, bf16[1,512,1024]{2,1,0:T(8,128)(2,1)} %narrow.9.refs_3_), custom_call_target="tpu_custom_call" | custom-call | bytes 12582912 | tf_op jit(solution)/shard_map/narrow/pallas_call | solution.py:84
  51.7 6.1 %narrow.11.refs_3_ = bf16[4,512,1024]{2,1,0:T(8,128)(2,1)} custom-call(s32[1]{0:T(128)} %bitcast.place_ref, f32[16,1024,1024]{2,1,0:T(8,128)} %w_ref.19, f32[13,2,1,512]{3,2,1,0:T(1,128)} %bitcast.16, f32[13,2,1,512]{3,2,1,0:T(1,128)} %bitcast.6.refs_2_.refs_1_, bf16[4,512,1024]{2,1,0:T(8,128)(2,1)} %narrow.10.refs_3_), custom_call_target="tpu_custom_call" | custom-call | bytes 12582912 | tf_op jit(solution)/shard_map/narrow/pallas_call | solution.py:84
  59.5 6.1 %narrow.12.refs_3_ = bf16[4,512,1024]{2,1,0:T(8,128)(2,1)} custom-call(s32[1]{0:T(128)} %bitcast.place_ref, f32[16,1024,1024]{2,1,0:T(8,128)} %w_ref.19, f32[13,2,1,512]{3,2,1,0:T(1,128)} %bitcast.17, f32[13,2,1,512]{3,2,1,0:T(1,128)} %bitcast.6.refs_2_.refs_1_, bf16[4,512,1024]{2,1,0:T(8,128)(2,1)} %narrow.11.refs_3_), custom_call_target="tpu_custom_call" | custom-call | bytes 12582912 | tf_op jit(solution)/shard_map/narrow/pallas_call | solution.py:84
  69.0 256.5 %collective-permute-done.10 = bf16[16,1024]{1,0:T(8,128)(2,1)S(1)} collective-permute-done((bf16[16,1024]{1,0:T(8,128)(2,1)S(1)}, bf16[16,1024]{1,0:T(8,128)(2,1)S(1)}, u32[]{:S(2)}, u32[]{:S(2)}) %collective-permute-start.10) | collective-permute-done | bytes 32800 | tf_op jit(solution)/shard_map/ppermute | solution.py:209
  326.4 21.5 %collective-permute-done.9.refs_2_ = bf16[1,512,1024]{2,1,0:T(8,128)(2,1)} collective-permute-done((bf16[1,512,1024]{2,1,0:T(8,128)(2,1)}, bf16[1,512,1024]{2,1,0:T(8,128)(2,1)}, u32[]{:S(2)}, u32[]{:S(2)}) %collective-permute-start.9) | collective-permute-done | bytes 1048608 | tf_op jit(solution)/shard_map/ppermute | solution.py:209
  348.4 2.9 narrow.13
  351.3 19.2 %collective-permute-done.8.refs_2_ = bf16[1,512,1024]{2,1,0:T(8,128)(2,1)} collective-permute-done((bf16[1,512,1024]{2,1,0:T(8,128)(2,1)}, bf16[1,512,1024]{2,1,0:T(8,128)(2,1)}, u32[]{:S(2)}, u32[]{:S(2)}) %collective-permute-start.8) | collective-permute-done | bytes 1048608 | tf_op jit(solution)/shard_map/ppermute | solution.py:209
  375.0 2.8 own.1.refs_3_
  377.8 16.6 %all_gather.3.router_ref = bf16[64,2048]{1,0:T(8,128)(2,1)} all-gather(bf16[16,2048]{1,0:T(8,128)(2,1)} %pad_maximum_fusion), channel_id=1, replica_groups=mesh['unit'=4,'ep'=4,'fsdp'=2] {'ep'}, dimensions={0}, use_global_device_ids=true | all-gather | bytes 327680 | tf_op jit(solution)/shard_map/all_gather | solution.py:276
  398.3 3.7 join.6.refs_3_
  402.0 3.7 join.7.refs_3_
  405.7 3.7 join.8.refs_3_
  409.4 8.6 %join.9.refs_3_ = bf16[16,512,2048]{2,1,0:T(8,128)(2,1)} custom-call(s32[1]{0:T(128)} %bitcast.place_ref, f32[16,1024,1024]{2,1,0:T(8,128)} %w_ref.19, f32[13,2,1,512]{3,2,1,0:T(1,128)} %bitcast.20, f32[13,2,1,512]{3,2,1,0:T(1,128)} %bitcast.6.refs_2_.refs_1_, bf16[4,512,1024]{2,1,0:T(8,128)(2,1)} %collective-permute-done.6.refs_2_, ...), custom_call_target="tpu_custom_call", output_to_operand_aliasing={{}: (5, {})} | custom-call | bytes 20971520 | tf_op jit(solution)/shard_map/join/pallas_call | solution.py:125
  418.0 8.6 %join.10.refs_3_ = bf16[16,512,2048]{2,1,0:T(8,128)(2,1)} custom-call(s32[1]{0:T(128)} %bitcast.place_ref, f32[16,1024,1024]{2,1,0:T(8,128)} %w_ref.19, f32[13,2,1,512]{3,2,1,0:T(1,128)} %bitcast.21, f32[13,2,1,512]{3,2,1,0:T(1,128)} %bitcast.6.refs_2_.refs_1_, bf16[4,512,1024]{2,1,0:T(8,128)(2,1)} %collective-permute-done.5.refs_2_, ...), custom_call_target="tpu_custom_call", output_to_operand_aliasing={{}: (5, {})} | custom-call | bytes 20971520 | tf_op jit(solution)/shard_map/join/pallas_call | solution.py:125
  426.5 8.6 %join.11.refs_0_ = bf16[16,512,2048]{2,1,0:T(8,128)(2,1)} custom-call(s32[1]{0:T(128)} %bitcast.place_ref, f32[16,1024,1024]{2,1,0:T(8,128)} %w_ref.19, f32[13,2,1,512]{3,2,1,0:T(1,128)} %bitcast.22, f32[13,2,1,512]{3,2,1,0:T(1,128)} %bitcast.6.refs_2_.refs_1_, bf16[4,512,1024]{2,1,0:T(8,128)(2,1)} %collective-permute-done.4.refs_2_, ...), custom_call_target="tpu_custom_call", output_to_operand_aliasing={{}: (5, {})} | custom-call | bytes 20971520 | tf_op jit(solution)/shard_map/join/pallas_call | solution.py:125
  435.1 2.3 lay.1
  (28 shorter events, 16.9 us)
Async XLA Ops:
  8.1 9.7 %collective-permute-start = (f32[2,1,1024]{2,1,0:T(1,128)}, f32[2,1,1024]{2,1,0:T(1,128)}, u32[]{:S(2)}, u32[]{:S(2)}) collective-permute-start(f32[2,1,1024]{2,1,0:T(1,128)} %sums.4), channel_id=1, source_target_pairs={{0,1},{1,0},{2,3},{3,2},{4,5},{5,4},{6,7},{7,6},{8,9},{9,8},{10,11... | collective-permute-start | bytes 24584 | tf_op jit(solution)/shard_map/ppermute | solution.py:209
  11.1 3.9 collective-permute-start.1
  40.7 4.5 %collective-permute-start.2 = (f32[13,1,1024]{2,1,0:T(1,128)}, f32[13,1,1024]{2,1,0:T(1,128)}, u32[]{:S(2)}, u32[]{:S(2)}) collective-permute-start(f32[13,1,1024]{2,1,0:T(1,128)} %sums.5.refs_4_), channel_id=1, source_target_pairs={{0,1},{1,0},{2,3},{3,2},{4,5},{5,4},{6,7},{7,6},{8,9},{9,8},{10,11... | collective-permute-start | bytes 159752 | tf_op jit(solution)/shard_map/ppermute | solution.py:209
  51.3 358.1 %collective-permute-start.6 = (bf16[4,512,1024]{2,1,0:T(8,128)(2,1)}, bf16[4,512,1024]{2,1,0:T(8,128)(2,1)}, u32[]{:S(2)}, u32[]{:S(2)}) collective-permute-start(bf16[4,512,1024]{2,1,0:T(8,128)(2,1)} %narrow.10.refs_3_), channel_id=1, source_target_pairs={{0,1},{1,0},{2,3},{3,2},{4,5},{5,4},{6,7},{7,6},{8,9},{9,8},{10,11... | collective-permute-start | bytes 12582920 | tf_op jit(solution)/shard_map/ppermute | solution.py:209
  57.9 360.1 %collective-permute-start.5 = (bf16[4,512,1024]{2,1,0:T(8,128)(2,1)}, bf16[4,512,1024]{2,1,0:T(8,128)(2,1)}, u32[]{:S(2)}, u32[]{:S(2)}) collective-permute-start(bf16[4,512,1024]{2,1,0:T(8,128)(2,1)} %narrow.11.refs_3_), channel_id=1, source_target_pairs={{0,1},{1,0},{2,3},{3,2},{4,5},{5,4},{6,7},{7,6},{8,9},{9,8},{10,11... | collective-permute-start | bytes 12582920 | tf_op jit(solution)/shard_map/ppermute | solution.py:209
  65.6 360.9 %collective-permute-start.4 = (bf16[4,512,1024]{2,1,0:T(8,128)(2,1)}, bf16[4,512,1024]{2,1,0:T(8,128)(2,1)}, u32[]{:S(2)}, u32[]{:S(2)}) collective-permute-start(bf16[4,512,1024]{2,1,0:T(8,128)(2,1)} %narrow.12.refs_3_), channel_id=1, source_target_pairs={{0,1},{1,0},{2,3},{3,2},{4,5},{5,4},{6,7},{7,6},{8,9},{9,8},{10,11... | collective-permute-start | bytes 12582920 | tf_op jit(solution)/shard_map/ppermute | solution.py:209
  66.9 258.6 %collective-permute-start.10 = (bf16[16,1024]{1,0:T(8,128)(2,1)S(1)}, bf16[16,1024]{1,0:T(8,128)(2,1)S(1)}, u32[]{:S(2)}, u32[]{:S(2)}) collective-permute-start(bf16[16,1024]{1,0:T(8,128)(2,1)S(1)} %fusion.2), channel_id=1, source_target_pairs={{0,1},{1,0},{2,3},{3,2},{4,5},{5,4},{6,7},{7,6},{8,9},{9,8},{10,11... | collective-permute-start | bytes 98312 | tf_op jit(solution)/shard_map/ppermute | solution.py:209
  68.5 279.5 %collective-permute-start.9 = (bf16[1,512,1024]{2,1,0:T(8,128)(2,1)}, bf16[1,512,1024]{2,1,0:T(8,128)(2,1)}, u32[]{:S(2)}, u32[]{:S(2)}) collective-permute-start(bf16[1,512,1024]{2,1,0:T(8,128)(2,1)} %narrow.7.refs_3_), channel_id=1, source_target_pairs={{0,1},{1,0},{2,3},{3,2},{4,5},{5,4},{6,7},{7,6},{8,9},{9,8},{10,11... | collective-permute-start | bytes 3145736 | tf_op jit(solution)/shard_map/ppermute | solution.py:209
  325.4 0.6 copy-start
  326.0 44.4 %collective-permute-start.8 = (bf16[1,512,1024]{2,1,0:T(8,128)(2,1)}, bf16[1,512,1024]{2,1,0:T(8,128)(2,1)}, u32[]{:S(2)}, u32[]{:S(2)}) collective-permute-start(bf16[1,512,1024]{2,1,0:T(8,128)(2,1)} %narrow.8.refs_0_.refs_3_), channel_id=1, source_target_pairs={{0,1},{1,0},{2,3},{3,2},{4,5},{5,4},{6,7},{7,6},{8,9},{9,8},{10,11... | collective-permute-start | bytes 3145736 | tf_op jit(solution)/shard_map/ppermute | solution.py:209
  348.0 57.7 %collective-permute-start.7 = (bf16[1,512,1024]{2,1,0:T(8,128)(2,1)}, bf16[1,512,1024]{2,1,0:T(8,128)(2,1)}, u32[]{:S(2)}, u32[]{:S(2)}) collective-permute-start(bf16[1,512,1024]{2,1,0:T(8,128)(2,1)} %narrow.9.refs_3_), channel_id=1, source_target_pairs={{0,1},{1,0},{2,3},{3,2},{4,5},{5,4},{6,7},{7,6},{8,9},{9,8},{10,11... | collective-permute-start | bytes 3145736 | tf_op jit(solution)/shard_map/ppermute | solution.py:209
  370.5 64.6 %collective-permute-start.3 = (bf16[1,512,1024]{2,1,0:T(8,128)(2,1)}, bf16[1,512,1024]{2,1,0:T(8,128)(2,1)}, u32[]{:S(2)}, u32[]{:S(2)}) collective-permute-start(bf16[1,512,1024]{2,1,0:T(8,128)(2,1)} %narrow.13), channel_id=1, source_target_pairs={{0,1},{1,0},{2,3},{3,2},{4,5},{5,4},{6,7},{7,6},{8,9},{9,8},{10,11... | collective-permute-start | bytes 3145736 | tf_op jit(solution)/shard_map/ppermute | solution.py:209
